TPU v7x, 128 devices: a whole 4x4x4 slice. The times are simulated.
128 devices in a mesh: dp: 8 (over z, core), mp: 16 (over x, y).
Axes of the slice: x: 4, y: 4, z: 4, core: 2. Of those that a mesh axis runs over, the one named last changes fastest.
Arguments:
- features: bfloat16 [8192, 2048], P('dp'), may hold values from -21 to 21
- rewards: float32 [32, 256], P('dp'), may hold values from -6 to 6
- old_values: float32 [32, 256], P('dp'), may hold values from -6 to 6
- dones: int32 [32, 256], P('dp'), may hold values 0 or 1
- lengths: int32 [32], P('dp'), may hold values from 128 to 256
- proj_weights: bfloat16 [2048, 2, 8192], P(None, None, 'mp'), may hold values from -0.125 to 0.125
- down_weight: bfloat16 [8192, 2048], P('mp'), may hold values from -0.0625 to 0.0625
- value_head: float32 [2048], replicated, may hold values from -0.0078125 to 0.0078125
- master: float32 [2048, 2, 8192], P('dp', None, 'mp'), may hold values from -0.125 to 0.125
- moment: float32 [2048, 2, 8192], P('dp', None, 'mp'), may hold values from -1.035801e-05 to 1.035801e-05
- second: float32 [2048, 2, 8192], P('dp', None, 'mp'), may hold values from 2.9802322e-13 to 2.9802322e-12
Outputs:
- master_new: float32 [2048, 2, 8192], P('dp', None, 'mp')
- moment_new: float32 [2048, 2, 8192], P('dp', None, 'mp')
- second_new: float32 [2048, 2, 8192], P('dp', None, 'mp')
- working: bfloat16 [2048, 2, 8192], P(None, None, 'mp')
- total_loss: float32 [], replicated
All inputs are finite; a program needn't handle non-finite values. No bound on the sum of `dones` on one device may be relied on, other than what follows from the above.
Results may differ from a plain program's by a relative error of at most 0.0011.
Values may be sent and summed in bfloat16 or wider, within the bound.
A program may use at most 128 MiB of HBM per device.

v0:
```python
import functools
import math
import jax
import jax.numpy as jnp
from jax import lax
from jax.sharding import Mesh
from jax.sharding import PartitionSpec as P

DP = ("dp_0", "dp_1")
MP = ("mp_0", "mp_1")
DP_MP = ("dp_0", "dp_1", "mp_0", "mp_1")
GAMMA = 0.99
LAMBDA = 0.95
MAX_NORM = 0.05


def own_block(parts, axes, sequence):
    shape = [lax.axis_size(a) for a in axes]
    parts = parts.reshape(*shape, *parts.shape[1:])
    parts = parts.transpose(*sequence, *range(len(axes), parts.ndim))
    parts = parts.reshape(-1, *parts.shape[len(axes) :])
    for k in sequence:
        parts = lax.psum_scatter(parts, axes[k], scatter_dimension=0, tiled=True)
    return parts[0]


def in_blocks(value, dim, count):
    before, after = (value.shape[:dim], value.shape[dim + 1 :])
    return jnp.moveaxis(value.reshape(*before, count, -1, *after), dim, 0)


def summed_rows(value, axes, sequence, dim):
    count = lax.axis_size(axes)
    return own_block(in_blocks(value, dim, count), axes, sequence)


def one_axis_at_a_time(value, axes):
    return functools.reduce(lax.psum, axes, value)


def gae_targets(rewards, old_values, dones, lengths):
    seq_len = rewards.shape[1]
    keeps = 1.0 - dones.astype(jnp.float32)
    following = jnp.concatenate([old_values[:, 1:], jnp.zeros_like(old_values[:, :1])], axis=1)
    deltas = rewards + GAMMA * following * keeps - old_values
    counted = jnp.cumsum(dones, axis=1) - dones
    places = jnp.arange(seq_len, dtype=jnp.int32)
    spans = places[None, :] - places[:, None]
    linked = (counted[:, :, None] == counted[:, None, :]) & (spans[None] >= 0)
    powers = jnp.exp(jnp.maximum(spans, 0).astype(jnp.float32) * math.log(GAMMA * LAMBDA))
    kernel = jnp.where(linked, powers[None], jnp.zeros((), jnp.float32))
    advantage = jnp.einsum("ats,as->at", kernel, deltas, precision=lax.Precision.HIGHEST)
    targets = (advantage + old_values).reshape(-1)
    mask = (places[None, :] < lengths[:, None]).astype(jnp.float32).reshape(-1)
    return (targets, mask)


def value_loss(features, mixed, targets, mask, value_head, total_tokens):
    stream = features.astype(jnp.float32) + mixed
    norm_factor = lax.rsqrt(jnp.mean(stream * stream, axis=-1) + 1e-05)
    normed = stream * norm_factor[:, None]
    estimate = jnp.dot(normed, value_head, precision=lax.Precision.HIGHEST)
    errors = estimate - targets
    loss_part = jnp.sum(mask * errors * errors) / total_tokens
    coeff = 2.0 * mask * errors / total_tokens
    head_grad = coeff[:, None] * value_head[None, :]
    out_grad = (
        norm_factor[:, None]
        * (head_grad - normed * jnp.mean(head_grad * normed, axis=-1, keepdims=True))
    ).astype(jnp.bfloat16)
    return (loss_part, out_grad)


def contract_rows(left, right):
    return lax.dot_general(
        left, right, (((0,), (0,)), ((), ())), preferred_element_type=jnp.float32
    )


def per_device(
    features,
    rewards,
    old_values,
    dones,
    lengths,
    proj_weights,
    down_weight,
    value_head,
    master,
    moment,
    second,
):
    token_count = features.shape[0]
    model_width = features.shape[1]
    ff_local = down_weight.shape[0]
    data_ways = lax.axis_size(DP)
    model_ways = lax.axis_size(MP)
    total_tokens = token_count * data_ways
    targets, mask = gae_targets(rewards, old_values, dones, lengths)
    both = jnp.dot(
        features,
        proj_weights.reshape(model_width, 2 * ff_local),
        preferred_element_type=jnp.float32,
    )
    both = both.reshape(token_count, 2, ff_local)
    gate_values = both[:, 0, :]
    up_values = both[:, 1, :]
    hidden = (jax.nn.silu(gate_values) * up_values).astype(jnp.bfloat16)
    mixed = lax.psum(
        jnp.dot(hidden, down_weight, preferred_element_type=jnp.float32).astype(jnp.bfloat16), MP
    ).astype(jnp.float32)
    loss_part, out_grad = value_loss(features, mixed, targets, mask, value_head, total_tokens)
    loss_part = loss_part / model_ways
    hidden_grad = jnp.dot(out_grad, down_weight.T, preferred_element_type=jnp.float32)
    gate_sigmoid = jax.nn.sigmoid(gate_values)
    gate_grad = (
        hidden_grad * up_values * gate_sigmoid * (1.0 + gate_values * (1.0 - gate_sigmoid))
    ).astype(jnp.bfloat16)
    up_grad = (hidden_grad * gate_values * gate_sigmoid).astype(jnp.bfloat16)
    both_grad = jnp.stack([gate_grad, up_grad], axis=1).reshape(token_count, 2 * ff_local)
    row_share = model_width // data_ways
    grads = summed_rows(
        contract_rows(features, both_grad).reshape(row_share * lax.axis_size(DP), 2, ff_local),
        DP,
        (1, 0),
        0,
    )
    squares = jnp.sum(grads * grads)
    squared_total, total_loss = (
        one_axis_at_a_time(squares, DP_MP),
        one_axis_at_a_time(loss_part, DP_MP),
    )
    clip = jnp.minimum(1.0, MAX_NORM / (jnp.sqrt(squared_total) + 1e-06))
    clipped = clip * grads
    moment_new = 0.9 * moment + 0.1 * clipped
    second_new = 0.999 * second + 0.001 * clipped * clipped
    first_hat = moment_new / (1.0 - 0.9**10)
    second_hat = second_new / (1.0 - 0.999**10)
    master_new = master - 0.001 * (first_hat / (jnp.sqrt(second_hat) + 1e-08) + 0.1 * master)
    working = lax.all_gather(master_new.astype(jnp.bfloat16), DP, axis=0, tiled=True)
    return (master_new, moment_new, second_new, working, total_loss)


def solution(mesh):
    finer = Mesh(mesh.devices.reshape(4, 2, 4, 4), ("dp_0", "dp_1", "mp_0", "mp_1"))
    return jax.shard_map(
        per_device,
        mesh=finer,
        in_specs=(
            P(DP, None),
            P(DP, None),
            P(DP, None),
            P(DP, None),
            P(DP),
            P(None, None, MP),
            P(MP, None),
            P(),
            P(DP, None, MP),
            P(DP, None, MP),
            P(DP, None, MP),
        ),
        out_specs=(P(DP, None, MP), P(DP, None, MP), P(DP, None, MP), P(None, None, MP), P()),
        check_vma=False,
    )
```

profile of v0, /device:TPU:1, one launch (start us, length us, event | category | flops | bytes accessed | tf_op | source)
XLA Modules:
  0.0 348.5 jit_solution(17223176488133655442)
XLA Ops:
  7.2 0.0 copy-start
  7.2 0.0 all-reduce.7.cloned.1.call-start
  7.2 5.5 %copy.34 = bf16[256,8,2,512]{3,1,2,0:T(8,128)(2,1)} copy(bf16[256,8,2,512]{3,2,1,0:T(2,128)(2,1)} %bitcast.73) | data formatting | bytes 8388608
  12.8 6.5 %copy.21 = bf16[1024,2048]{1,0:T(8,128)(2,1)} copy(bf16[1024,2048]{0,1:T(8,128)(2,1)} %bitcast.72) | data formatting | bytes 8388608 | tf_op jit(solution)/shard_map/dot_general | solution.py:100
  19.3 7.6 %fusion.6 = f32[1024,2,512]{0,2,1:T(8,128)S(1)} fusion(bf16[2,512,2048]{2,1,0:T(8,128)(2,1)} %bitcast.74, bf16[1024,2048]{1,0:T(8,128)(2,1)} %param.11), kind=kOutput, calls=%fused_computation.10 | convolution fusion | flops 4294967296 | bytes 12582912 | tf_op jit(solution)/shard_map/dot_general | solution.py:100
  26.9 0.0 copy-start.9
  26.9 2.0 copy-done.9
  28.9 0.0 copy-done
  28.9 4.4 %convolution_convert_fusion = bf16[1024,2048]{1,0:T(8,128)(2,1)} fusion(bf16[512,2048]{1,0:T(8,128)(2,1)S(1)} %copy-done, f32[1024,2,512]{0,2,1:T(8,128)S(1)} %fusion.6), kind=kOutput, calls=%fused_computation.14 | convolution fusion | flops 2152726528 | bytes 10485760 | tf_op jit(solution)/shard_map/dot_general | solution.py:110
  33.3 0.0 copy-start.8
  33.3 0.0 copy-start.5
  33.3 0.0 copy-start.4
  33.3 0.0 all-reduce.7.cloned.1.call-update
  33.4 0.2 reduce-scatter.3.cloned.1.call-start
  33.6 0.4 copy-done.8
  34.0 0.1 iota_compare_fusion
  34.1 0.0 copy-done.5
  34.1 0.1 slice.19
  34.1 0.0 copy-done.4
  34.2 1.2 reduce-window.6
  35.4 0.1 slice.22
  35.4 0.1 copy.22
  35.6 0.1 copy.23
  35.7 0.1 multiply_exponential_fusion
  35.8 0.1 add_bitcast_fusion
  35.9 0.0 copy-done.7
  35.9 1.2 fusion.13
  37.1 0.0 copy-start.6
  37.1 102.5 %all-reduce.7.cloned.1.call-done = bf16[1024,2048]{1,0:T(8,128)(2,1)} async-done(((bf16[1024,2048]{1,0:T(8,128)(2,1)}), bf16[1024,2048]{1,0:T(8,128)(2,1)}) %all-reduce.7.cloned.1.call-update) | async-done | bytes 4194320 | tf_op jit(solution)/shard_map/psum | solution.py:109
  139.7 0.0 copy-start.2
  139.7 0.0 copy-start.3
  139.7 5.0 %multiply_reduce_fusion = f32[1024]{0:T(1024)S(1)} fusion(bf16[1024,2048]{1,0:T(8,128)(2,1)} %all-reduce.7.cloned.1.call-done, bf16[1024,2048]{1,0:T(8,128)(2,1)} %param.11), kind=kLoop, calls=%fused_computation.5 | loop fusion | flops 10484736 | bytes 8392704 | tf_op jit(solution)/shard_map/reduce_sum | solution.py:60
  144.7 0.0 copy-done.6
  144.7 0.0 copy-done.2
  144.7 0.9 copy-done.3
  145.6 8.1 %fusion.4 = f32[1,1024]{1,0:T(1,128)S(1)} fusion(f32[2048,1]{0,1:T(1,128)S(1)} %bitcast.76, bf16[1024,2048]{1,0:T(8,128)(2,1)S(1)} %copy-done.3, bf16[1024,2048]{1,0:T(8,128)(2,1)S(1)} %copy-done.2, f32[1024]{0:T(1024)S(1)} %add_rsqrt_fusion), kind=kOutput, calls=%fused_computation.8 | convolution fusion | flops 33554432 | bytes 8404992 | tf_op jit(solution)/shard_map/dot_general | solution.py:62
  153.7 0.6 fusion.26
  154.4 2.6 fusion
  156.9 0.0 copy-done.10
  156.9 5.4 %fusion.19 = (bf16[1024,1,512]{0,2,1:T(8,128)(2,1)S(1)}, bf16[1024,1,512]{0,2,1:T(8,128)(2,1)S(1)}) fusion(f32[1024,2,512]{0,2,1:T(8,128)S(1)} %copy-done.10, bf16[512,2048]{1,0:T(8,128)(2,1)S(1)} %copy-done, bf16[1024,2048]{1,0:T(8,128)(2,1)S(1)} %copy-done.3, bf16[1024,2048]{1,0:T(8,128)(2,1)S(1)} %copy-done.2, f32[1024]{0:T(1024)S(1)} %broadcast_multiply_fusion, ...), kind=kOutput, calls=%fused_computation.36 | convolution fusion | flops 2173173760 | bytes 16797696 | tf_op jit(solution)/shard_map/dot_general | solution.py:114
  162.4 0.2 pad_maximum_fusion
  162.6 6.7 %convolution_bitcast_fusion = f32[2048,1024]{0,1:T(8,128)} fusion(bf16[1024,1024]{0,1:T(8,128)(2,1)S(1)} %bitcast.75, bf16[1024,2048]{1,0:T(8,128)(2,1)S(1)} %copy-done.2), kind=kOutput, calls=%fused_computation.9 | convolution fusion | flops 4294967296 | bytes 14680064 | tf_op jit(solution)/shard_map/dot_general | solution.py:75
  169.3 11.7 %reshape_reshape_reshape.3 = f32[4,2,256,2,512]{2,1,0,4,3:T(2,128)} reshape(f32[2048,1024]{0,1:T(8,128)} %convolution_bitcast_fusion) | data formatting | bytes 16777216 | tf_op jit(solution)/shard_map/reshape;reshape;reshape | solution.py:19
  181.0 13.1 %copy.24 = f32[2,4,256,2,512]{4,2,3,1,0:T(8,128)} copy(f32[2,4,256,2,512]{2,0,1,4,3:T(2,128)} %bitcast.71) | data formatting | bytes 16777216 | tf_op jit(solution)/shard_map/transpose | solution.py:20
  194.1 0.0 reduce-scatter.3.cloned.1.call-update
  194.1 0.0 reduce-scatter.5.cloned.1.call-start
  194.2 19.7 %reduce-scatter.3.cloned.1.call-done = f32[4,256,2,512]{3,1,2,0:T(8,128)} async-done(((f32[8,256,2,512]{3,1,2,0:T(8,128)}), f32[4,256,2,512]{3,1,2,0:T(8,128)}) %reduce-scatter.3.cloned.1.call-update) | async-done | bytes 4194320 | tf_op jit(solution)/shard_map/reduce_scatter | solution.py:23
  213.9 0.0 reduce-scatter.5.cloned.1.call-update
  213.9 0.0 all-gather.2.cloned.1.call-start
  214.6 49.8 %reduce-scatter.5.cloned.1.call-done = f32[1,256,2,512]{3,1,2,0:T(8,128)} async-done(((f32[4,256,2,512]{3,1,2,0:T(8,128)}), f32[1,256,2,512]{3,1,2,0:T(8,128)}) %reduce-scatter.5.cloned.1.call-update) | async-done | bytes 1048592 | tf_op jit(solution)/shard_map/reduce_scatter | solution.py:23
  264.4 2.1 multiply_reduce_fusion.1
  266.5 7.1 %all-reduce.3 = (f32[]{:T(128)}, f32[]{:T(128)}) all-reduce(f32[]{:T(128)} %multiply_reduce_fusion.1, f32[]{:T(128)S(6)} %div.55), channel_id=1, replica_groups=mesh['dp_0'=4,'dp_1'=2,'mp_0'=4,'mp_1'=4] {'dp_0'}, use_global_device_ids=true, to_apply=%region_8.9 | all-reduce | flops 2 | bytes 16 | tf_op jit(solution)/shard_map/psum | solution.py:38
  273.6 5.5 %all-reduce.4 = (f32[]{:T(128)}, f32[]{:T(128)}) all-reduce(f32[]{:T(128)} %get-tuple-element.14, f32[]{:T(128)} %get-tuple-element.15), channel_id=1, replica_groups=mesh['dp_0'=4,'dp_1'=2,'mp_0'=4,'mp_1'=4] {'dp_1'}, use_global_device_ids=true, to_apply=%region_9.10 | all-reduce | flops 2 | bytes 16 | tf_op jit(solution)/shard_map/psum | solution.py:38
  279.1 9.0 %all-reduce.2 = (f32[]{:T(128)}, f32[]{:T(128)}) all-reduce(f32[]{:T(128)} %get-tuple-element.16, f32[]{:T(128)} %get-tuple-element.17), channel_id=1, replica_groups=mesh['dp_0'=4,'dp_1'=2,'mp_0'=4,'mp_1'=4] {'mp_0'}, use_global_device_ids=true, to_apply=%region_10.11 | all-reduce | flops 2 | bytes 16 | tf_op jit(solution)/shard_map/psum | solution.py:38
  288.1 9.1 %all-reduce.1 = (f32[]{:T(128)}, f32[]{:T(128)}) all-reduce(f32[]{:T(128)} %get-tuple-element.12, f32[]{:T(128)} %get-tuple-element.13), channel_id=1, replica_groups=mesh['dp_0'=4,'dp_1'=2,'mp_0'=4,'mp_1'=4] {'mp_1'}, use_global_device_ids=true, to_apply=%region_11.12 | all-reduce | flops 2 | bytes 16 | tf_op jit(solution)/shard_map/psum | solution.py:38
  297.9 3.2 fusion.31
  301.1 1.3 copy.28
  302.4 0.0 all-gather.2.cloned.1.call-update
  302.5 1.8 copy.29
  304.2 1.8 copy.30
  306.0 1.8 copy.31
  307.8 26.3 %all-gather.2.cloned.1.call-done = bf16[2048,2,512]{2,1,0:T(2,128)(2,1)} async-done(((bf16[256,2,512]{2,1,0:T(2,128)(2,1)}), bf16[2048,2,512]{2,1,0:T(2,128)(2,1)}) %all-gather.2.cloned.1.call-update) | async-done | bytes 4194320 | tf_op jit(solution)/shard_map/all_gather | solution.py:140
  334.1 7.8 %copy.53 = bf16[2048,2,512]{2,1,0:T(2,128)(2,1)} copy(bf16[2048,2,512]{2,1,0:T(2,128)(2,1)} %all-gather.2.cloned.1.call-done) | data formatting | bytes 8388608
  341.9 0.0 copy-done.1
  (14 shorter events, 0.2 us)
Async XLA Ops:
  7.2 21.7 %copy-start = (bf16[512,2048]{1,0:T(8,128)(2,1)S(1)}, bf16[512,2048]{1,0:T(8,128)(2,1)}, u32[]{:S(2)}) copy-start(bf16[512,2048]{1,0:T(8,128)(2,1)} %param.17) | copy-start | bytes 6291460
  7.2 132.5 %all-reduce.7.cloned.1.call-start = ((), (), s32[]{:S(2)}) async-start(), calls=%async_computation.2 | async-start | bytes 8388608 | tf_op jit(solution)/shard_map/psum | solution.py:109
  26.9 2.0 copy-start.9
  33.3 0.7 copy-start.8
  33.3 0.7 copy-start.5
  33.3 0.8 copy-start.4
  33.3 2.5 copy-start.7
  33.4 180.5 %reduce-scatter.3.cloned.1.call-start = ((), (), s32[]{:S(2)}) async-start(), calls=%async_computation.3 | async-start | bytes 12582912 | tf_op jit(solution)/shard_map/reduce_scatter | solution.py:23
  37.1 107.6 %copy-start.6 = (f32[2048]{0:T(1024)S(1)}, f32[2048]{0:T(1024)}, u32[]{:S(2)}) copy-start(f32[2048]{0:T(1024)} %param.18) | copy-start | bytes 24580
  139.7 5.1 %copy-start.2 = (bf16[1024,2048]{1,0:T(8,128)(2,1)S(1)}, bf16[1024,2048]{1,0:T(8,128)(2,1)}, u32[]{:S(2)}) copy-start(bf16[1024,2048]{1,0:T(8,128)(2,1)} %param.11) | copy-start | bytes 12582916
  139.7 5.9 %copy-start.3 = (bf16[1024,2048]{1,0:T(8,128)(2,1)S(1)}, bf16[1024,2048]{1,0:T(8,128)(2,1)}, u32[]{:S(2)}) copy-start(bf16[1024,2048]{1,0:T(8,128)(2,1)} %all-reduce.7.cloned.1.call-done) | copy-start | bytes 12582916
  154.3 2.6 copy-start.10
  194.1 70.3 %reduce-scatter.5.cloned.1.call-start = ((), (), s32[]{:S(2)}) async-start(), calls=%async_computation.4 | async-start | bytes 5242880 | tf_op jit(solution)/shard_map/reduce_scatter | solution.py:23
  213.9 120.2 %all-gather.2.cloned.1.call-start = ((), (), s32[]{:S(2)}) async-start(), calls=%async_computation.5 | async-start | bytes 4718592 | tf_op jit(solution)/shard_map/all_gather | solution.py:140
  334.1 7.9 %copy-start.1 = (bf16[512,2048]{1,0:T(8,128)(2,1)S(1)}, bf16[512,2048]{1,0:T(8,128)(2,1)}, u32[]{:S(2)}) copy-start(bf16[512,2048]{1,0:T(8,128)(2,1)} %param.17) | copy-start | bytes 6291460
Sparse Core Ops, SparseCore 0:
  33.5 106.1 all-reduce.6
  194.2 19.5 reduce-scatter.2
  216.3 48.0 reduce-scatter.4
  302.6 31.4 all-gather.1
where the time goes:
time: 350 us; the launch traced here: 348 us
  waiting for transfers between devices  198 us (57%)
  local copies, waits for them, and re-layouts  55.1 us (16%)
  matrix products  33.5 us (10%)
  blocking collectives  30.7 us (9%)
  other arithmetic  15.3 us (4%)
  between operations  15.3 us (4%)
    psum x1, waiting for transfers between devices, per_device(): lax.psum(jnp.dot(hidden, down_weight, preferred_element_type=jnp.float32)...  103 us
    reduce_scatter x2, waiting for transfers between devices, own_block(): parts = lax.psum_scatter(parts, axes[k], scatter_dimension=0, tiled=True)  69.5 us
    psum x4, blocking collectives, one_axis_at_a_time(): return functools.reduce(lax.psum, axes, value)  30.7 us
    all_gather x1, waiting for transfers between devices, per_device(): lax.all_gather(master_new.astype(jnp.bfloat16), DP, axis=0, tiled=True)  26.3 us
    unnamed x28, local copies, waits for them, and re-layouts  22 us
    transpose x1, local copies, waits for them, and re-layouts, own_block(): parts = parts.transpose(*sequence, *range(len(axes), parts.ndim))  13.1 us
    another operation x1, local copies, waits for them, and re-layouts, own_block(): parts = parts.reshape(*shape, *parts.shape[1:])  11.7 us
    dot_general x1, matrix products, value_loss(): estimate = jnp.dot(normed, value_head, precision=lax.Precision.HIGHEST)  8.13 us
  transfers between devices with their start and end apart: 4, of which 4 were waited for; matrix products, arithmetic and copies ran while one was open for 2% of the time, Pallas kernels for 0%

commit v1 on v0

--- a/solution.py
+++ b/solution.py
@@ -137,7 +137,9 @@
     first_hat = moment_new / (1.0 - 0.9**10)
     second_hat = second_new / (1.0 - 0.999**10)
     master_new = master - 0.001 * (first_hat / (jnp.sqrt(second_hat) + 1e-08) + 0.1 * master)
-    working = lax.all_gather(master_new.astype(jnp.bfloat16), DP, axis=0, tiled=True)
+    x = master_new.astype(jnp.bfloat16)
+    sent = jnp.stack([x] * lax.axis_size(DP))
+    working = jnp.concatenate(lax.all_to_all(sent, DP, 0, 0), axis=0)
     return (master_new, moment_new, second_new, working, total_loss)
 
 

time: 350 us -> 379 us (1.083)
  waiting for transfers between devices: 198 us -> 216 us
  starting transfers between devices: 0.34 us -> 9.1 us
    all_to_all x0 -> x1, waiting for transfers between devices: none -> 43.5 us  [per_device(): working = jnp.concatenate(lax.all_to_all(sent, DP, 0, 0), axis=0)]
    all_gather x1 -> x0, waiting for transfers between devices: 26.3 us -> none  [per_device(): lax.all_gather(master_new.astype(jnp.bfloat16), DP, axis=0, tiled=True)]
    all_to_all x0 -> x1, starting transfers between devices: none -> 8.8 us  [per_device(): working = jnp.concatenate(lax.all_to_all(sent, DP, 0, 0), axis=0)]
    another operation x2 -> x3, local copies, waits for them, and re-layouts: 0.1 us -> 4.27 us  [the longest x1 4.17 us: per_device(): sent = jnp.stack([x] * lax.axis_size(DP))]
where the time goes in v1:
time: 379 us; the launch traced here: 378 us
  waiting for transfers between devices  216 us (57%)
  local copies, waits for them, and re-layouts  58.4 us (15%)
  matrix products  33.5 us (9%)
  blocking collectives  30.7 us (8%)
  other arithmetic  15.3 us (4%)
  between operations  15.3 us (4%)
  starting transfers between devices  9.1 us (2%)
    psum x1, waiting for transfers between devices, per_device(): lax.psum(jnp.dot(hidden, down_weight, preferred_element_type=jnp.float32)...  103 us
    reduce_scatter x2, waiting for transfers between devices, own_block(): parts = lax.psum_scatter(parts, axes[k], scatter_dimension=0, tiled=True)  69.5 us
    all_to_all x1, waiting for transfers between devices, per_device(): working = jnp.concatenate(lax.all_to_all(sent, DP, 0, 0), axis=0)  43.5 us
    psum x4, blocking collectives, one_axis_at_a_time(): return functools.reduce(lax.psum, axes, value)  30.7 us
    unnamed x28, local copies, waits for them, and re-layouts  22 us
    transpose x1, local copies, waits for them, and re-layouts, own_block(): parts = parts.transpose(*sequence, *range(len(axes), parts.ndim))  13.1 us
    another operation x1, local copies, waits for them, and re-layouts, own_block(): parts = parts.reshape(*shape, *parts.shape[1:])  11.7 us
    all_to_all x1, starting transfers between devices, per_device(): working = jnp.concatenate(lax.all_to_all(sent, DP, 0, 0), axis=0)  8.8 us
  transfers between devices with their start and end apart: 4, of which 4 were waited for; matrix products, arithmetic and copies ran while one was open for 2% of the time, Pallas kernels for 0%

profile of v1, /device:TPU:1, one launch (start us, length us, event | category | flops | bytes accessed | tf_op | source)
XLA Modules:
  0.0 377.8 jit_solution(431358957323541272)
XLA Ops:
  7.2 0.0 copy-start
  7.2 0.0 all-reduce.7.cloned.1.call-start
  7.2 5.5 %copy.34 = bf16[256,8,2,512]{3,1,2,0:T(8,128)(2,1)} copy(bf16[256,8,2,512]{3,2,1,0:T(2,128)(2,1)} %bitcast.74) | data formatting | bytes 8388608
  12.8 6.5 %copy.21 = bf16[1024,2048]{1,0:T(8,128)(2,1)} copy(bf16[1024,2048]{0,1:T(8,128)(2,1)} %bitcast.73) | data formatting | bytes 8388608 | tf_op jit(solution)/shard_map/dot_general | solution.py:100
  19.3 7.6 %fusion.6 = f32[1024,2,512]{0,2,1:T(8,128)S(1)} fusion(bf16[2,512,2048]{2,1,0:T(8,128)(2,1)} %bitcast.75, bf16[1024,2048]{1,0:T(8,128)(2,1)} %param.11), kind=kOutput, calls=%fused_computation.10 | convolution fusion | flops 4294967296 | bytes 12582912 | tf_op jit(solution)/shard_map/dot_general | solution.py:100
  26.9 0.0 copy-start.9
  26.9 2.0 copy-done.9
  28.9 0.0 copy-done
  28.9 4.4 %convolution_convert_fusion = bf16[1024,2048]{1,0:T(8,128)(2,1)} fusion(bf16[512,2048]{1,0:T(8,128)(2,1)S(1)} %copy-done, f32[1024,2,512]{0,2,1:T(8,128)S(1)} %fusion.6), kind=kOutput, calls=%fused_computation.14 | convolution fusion | flops 2152726528 | bytes 10485760 | tf_op jit(solution)/shard_map/dot_general | solution.py:110
  33.3 0.0 copy-start.8
  33.3 0.0 copy-start.5
  33.3 0.0 copy-start.4
  33.3 0.0 all-reduce.7.cloned.1.call-update
  33.4 0.2 reduce-scatter.3.cloned.1.call-start
  33.6 0.4 copy-done.8
  34.0 0.1 iota_compare_fusion
  34.1 0.0 copy-done.5
  34.1 0.1 slice.19
  34.1 0.0 copy-done.4
  34.2 1.2 reduce-window.6
  35.4 0.1 slice.22
  35.4 0.1 copy.22
  35.6 0.1 copy.23
  35.7 0.1 multiply_exponential_fusion
  35.8 0.1 add_bitcast_fusion
  35.9 0.0 copy-done.7
  35.9 1.2 fusion.13
  37.1 0.0 copy-start.6
  37.1 102.5 %all-reduce.7.cloned.1.call-done = bf16[1024,2048]{1,0:T(8,128)(2,1)} async-done(((bf16[1024,2048]{1,0:T(8,128)(2,1)}), bf16[1024,2048]{1,0:T(8,128)(2,1)}) %all-reduce.7.cloned.1.call-update) | async-done | bytes 4194320 | tf_op jit(solution)/shard_map/psum | solution.py:109
  139.7 0.0 copy-start.2
  139.7 0.0 copy-start.3
  139.7 5.0 %multiply_reduce_fusion = f32[1024]{0:T(1024)S(1)} fusion(bf16[1024,2048]{1,0:T(8,128)(2,1)} %all-reduce.7.cloned.1.call-done, bf16[1024,2048]{1,0:T(8,128)(2,1)} %param.11), kind=kLoop, calls=%fused_computation.5 | loop fusion | flops 10484736 | bytes 8392704 | tf_op jit(solution)/shard_map/reduce_sum | solution.py:60
  144.7 0.0 copy-done.6
  144.7 0.0 copy-done.2
  144.7 0.9 copy-done.3
  145.6 8.1 %fusion.4 = f32[1,1024]{1,0:T(1,128)S(1)} fusion(f32[2048,1]{0,1:T(1,128)S(1)} %bitcast.77, bf16[1024,2048]{1,0:T(8,128)(2,1)S(1)} %copy-done.3, bf16[1024,2048]{1,0:T(8,128)(2,1)S(1)} %copy-done.2, f32[1024]{0:T(1024)S(1)} %add_rsqrt_fusion), kind=kOutput, calls=%fused_computation.8 | convolution fusion | flops 33554432 | bytes 8404992 | tf_op jit(solution)/shard_map/dot_general | solution.py:62
  153.7 0.6 fusion.26
  154.4 2.6 fusion
  156.9 0.0 copy-done.10
  156.9 5.4 %fusion.19 = (bf16[1024,1,512]{0,2,1:T(8,128)(2,1)S(1)}, bf16[1024,1,512]{0,2,1:T(8,128)(2,1)S(1)}) fusion(f32[1024,2,512]{0,2,1:T(8,128)S(1)} %copy-done.10, bf16[512,2048]{1,0:T(8,128)(2,1)S(1)} %copy-done, bf16[1024,2048]{1,0:T(8,128)(2,1)S(1)} %copy-done.3, bf16[1024,2048]{1,0:T(8,128)(2,1)S(1)} %copy-done.2, f32[1024]{0:T(1024)S(1)} %broadcast_multiply_fusion, ...), kind=kOutput, calls=%fused_computation.36 | convolution fusion | flops 2173173760 | bytes 16797696 | tf_op jit(solution)/shard_map/dot_general | solution.py:114
  162.4 0.2 pad_maximum_fusion
  162.6 6.7 %convolution_bitcast_fusion = f32[2048,1024]{0,1:T(8,128)} fusion(bf16[1024,1024]{0,1:T(8,128)(2,1)S(1)} %bitcast.76, bf16[1024,2048]{1,0:T(8,128)(2,1)S(1)} %copy-done.2), kind=kOutput, calls=%fused_computation.9 | convolution fusion | flops 4294967296 | bytes 14680064 | tf_op jit(solution)/shard_map/dot_general | solution.py:75
  169.3 11.7 %reshape_reshape_reshape.3 = f32[4,2,256,2,512]{2,1,0,4,3:T(2,128)} reshape(f32[2048,1024]{0,1:T(8,128)} %convolution_bitcast_fusion) | data formatting | bytes 16777216 | tf_op jit(solution)/shard_map/reshape;reshape;reshape | solution.py:19
  181.0 13.1 %copy.24 = f32[2,4,256,2,512]{4,2,3,1,0:T(8,128)} copy(f32[2,4,256,2,512]{2,0,1,4,3:T(2,128)} %bitcast.72) | data formatting | bytes 16777216 | tf_op jit(solution)/shard_map/transpose | solution.py:20
  194.1 0.0 reduce-scatter.3.cloned.1.call-update
  194.1 0.0 reduce-scatter.5.cloned.1.call-start
  194.2 19.7 %reduce-scatter.3.cloned.1.call-done = f32[4,256,2,512]{3,1,2,0:T(8,128)} async-done(((f32[8,256,2,512]{3,1,2,0:T(8,128)}), f32[4,256,2,512]{3,1,2,0:T(8,128)}) %reduce-scatter.3.cloned.1.call-update) | async-done | bytes 4194320 | tf_op jit(solution)/shard_map/reduce_scatter | solution.py:23
  213.9 0.0 reduce-scatter.5.cloned.1.call-update
  214.5 49.8 %reduce-scatter.5.cloned.1.call-done = f32[1,256,2,512]{3,1,2,0:T(8,128)} async-done(((f32[4,256,2,512]{3,1,2,0:T(8,128)}), f32[1,256,2,512]{3,1,2,0:T(8,128)}) %reduce-scatter.5.cloned.1.call-update) | async-done | bytes 1048592 | tf_op jit(solution)/shard_map/reduce_scatter | solution.py:23
  264.4 2.1 multiply_reduce_fusion.1
  266.5 7.1 %all-reduce.3 = (f32[]{:T(128)}, f32[]{:T(128)}) all-reduce(f32[]{:T(128)} %multiply_reduce_fusion.1, f32[]{:T(128)S(6)} %div.55), channel_id=1, replica_groups=mesh['dp_0'=4,'dp_1'=2,'mp_0'=4,'mp_1'=4] {'dp_0'}, use_global_device_ids=true, to_apply=%region_8.9 | all-reduce | flops 2 | bytes 16 | tf_op jit(solution)/shard_map/psum | solution.py:38
  273.6 5.5 %all-reduce.4 = (f32[]{:T(128)}, f32[]{:T(128)}) all-reduce(f32[]{:T(128)} %get-tuple-element.14, f32[]{:T(128)} %get-tuple-element.15), channel_id=1, replica_groups=mesh['dp_0'=4,'dp_1'=2,'mp_0'=4,'mp_1'=4] {'dp_1'}, use_global_device_ids=true, to_apply=%region_9.10 | all-reduce | flops 2 | bytes 16 | tf_op jit(solution)/shard_map/psum | solution.py:38
  279.1 9.0 %all-reduce.2 = (f32[]{:T(128)}, f32[]{:T(128)}) all-reduce(f32[]{:T(128)} %get-tuple-element.16, f32[]{:T(128)} %get-tuple-element.17), channel_id=1, replica_groups=mesh['dp_0'=4,'dp_1'=2,'mp_0'=4,'mp_1'=4] {'mp_0'}, use_global_device_ids=true, to_apply=%region_10.11 | all-reduce | flops 2 | bytes 16 | tf_op jit(solution)/shard_map/psum | solution.py:38
  288.1 9.1 %all-reduce.1 = (f32[]{:T(128)}, f32[]{:T(128)}) all-reduce(f32[]{:T(128)} %get-tuple-element.12, f32[]{:T(128)} %get-tuple-element.13), channel_id=1, replica_groups=mesh['dp_0'=4,'dp_1'=2,'mp_0'=4,'mp_1'=4] {'mp_1'}, use_global_device_ids=true, to_apply=%region_11.12 | all-reduce | flops 2 | bytes 16 | tf_op jit(solution)/shard_map/psum | solution.py:38
  297.9 3.2 fusion.31
  301.1 0.5 copy.28
  301.7 4.2 %stack.11 = bf16[8,256,2,512]{3,2,1,0:T(2,128)(2,1)} broadcast(bf16[256,2,512]{2,1,0:T(2,128)(2,1)S(1)} %copy.28), dimensions={1,2,3} | broadcast | bytes 4718592 | tf_op jit(solution)/shard_map/stack | solution.py:141
  305.8 8.8 %all-to-all-start = ((bf16[8,256,2,512]{3,2,1,0:T(2,128)(2,1)}), bf16[8,256,2,512]{3,2,1,0:T(2,128)(2,1)}, u32[]{:S(2)}, u32[]{:S(2)}) async-start(bf16[8,256,2,512]{3,2,1,0:T(2,128)(2,1)} %stack.11), calls=%async_computation.2 | async-start | bytes 8388608 | tf_op jit(solution)/shard_map/all_to_all | solution.py:142
  314.6 1.8 copy.29
  316.4 1.8 copy.30
  318.2 1.8 copy.31
  320.0 43.5 %all-to-all-done = bf16[8,256,2,512]{3,2,1,0:T(2,128)(2,1)} async-done(((bf16[8,256,2,512]{3,2,1,0:T(2,128)(2,1)}), bf16[8,256,2,512]{3,2,1,0:T(2,128)(2,1)}, u32[]{:S(2)}, u32[]{:S(2)}) %all-to-all-start) | async-done | bytes 4194336 | tf_op jit(solution)/shard_map/all_to_all | solution.py:142
  363.4 7.8 %copy.53 = bf16[2048,2,512]{2,1,0:T(2,128)(2,1)} copy(bf16[2048,2,512]{2,1,0:T(2,128)(2,1)} %bitcast.17) | data formatting | bytes 8388608
  371.3 0.0 copy-done.1
  (14 shorter events, 0.2 us)
Async XLA Ops:
  7.2 21.7 %copy-start = (bf16[512,2048]{1,0:T(8,128)(2,1)S(1)}, bf16[512,2048]{1,0:T(8,128)(2,1)}, u32[]{:S(2)}) copy-start(bf16[512,2048]{1,0:T(8,128)(2,1)} %param.17) | copy-start | bytes 6291460
  7.2 132.5 %all-reduce.7.cloned.1.call-start = ((), (), s32[]{:S(2)}) async-start(), calls=%async_computation.3 | async-start | bytes 8388608 | tf_op jit(solution)/shard_map/psum | solution.py:109
  26.9 2.0 copy-start.9
  33.3 0.7 copy-start.8
  33.3 0.7 copy-start.5
  33.3 0.8 copy-start.4
  33.3 2.5 copy-start.7
  33.4 180.5 %reduce-scatter.3.cloned.1.call-start = ((), (), s32[]{:S(2)}) async-start(), calls=%async_computation.4 | async-start | bytes 12582912 | tf_op jit(solution)/shard_map/reduce_scatter | solution.py:23
  37.1 107.6 %copy-start.6 = (f32[2048]{0:T(1024)S(1)}, f32[2048]{0:T(1024)}, u32[]{:S(2)}) copy-start(f32[2048]{0:T(1024)} %param.18) | copy-start | bytes 24580
  139.7 5.1 %copy-start.2 = (bf16[1024,2048]{1,0:T(8,128)(2,1)S(1)}, bf16[1024,2048]{1,0:T(8,128)(2,1)}, u32[]{:S(2)}) copy-start(bf16[1024,2048]{1,0:T(8,128)(2,1)} %param.11) | copy-start | bytes 12582916
  139.7 5.9 %copy-start.3 = (bf16[1024,2048]{1,0:T(8,128)(2,1)S(1)}, bf16[1024,2048]{1,0:T(8,128)(2,1)}, u32[]{:S(2)}) copy-start(bf16[1024,2048]{1,0:T(8,128)(2,1)} %all-reduce.7.cloned.1.call-done) | copy-start | bytes 12582916
  154.3 2.6 copy-start.10
  194.1 70.3 %reduce-scatter.5.cloned.1.call-start = ((), (), s32[]{:S(2)}) async-start(), calls=%async_computation.5 | async-start | bytes 5242880 | tf_op jit(solution)/shard_map/reduce_scatter | solution.py:23
  305.8 57.6 %all-to-all-start = ((bf16[8,256,2,512]{3,2,1,0:T(2,128)(2,1)}), bf16[8,256,2,512]{3,2,1,0:T(2,128)(2,1)}, u32[]{:S(2)}, u32[]{:S(2)}) async-start(bf16[8,256,2,512]{3,2,1,0:T(2,128)(2,1)} %stack.11), calls=%async_computation.2 | async-start | bytes 8388608 | tf_op jit(solution)/shard_map/all_to_all | solution.py:142
  363.4 7.9 %copy-start.1 = (bf16[512,2048]{1,0:T(8,128)(2,1)S(1)}, bf16[512,2048]{1,0:T(8,128)(2,1)}, u32[]{:S(2)}) copy-start(bf16[512,2048]{1,0:T(8,128)(2,1)} %param.17) | copy-start | bytes 6291460
Sparse Core Ops, SparseCore 0:
  33.5 106.1 all-reduce.6
  194.2 19.5 reduce-scatter.2
  216.3 48.0 reduce-scatter.4
